TPU v7x, 16 devices: a whole 2x2x2 slice. The times are simulated.
16 devices in a mesh: col: 4 (over z, y), row: 4 (over x, core).
Axes of the slice: x: 2, y: 2, z: 2, core: 2. Of those that a mesh axis runs over, the one named last changes fastest.
Arguments:
- t_amp: float32 [256, 20736], P('row', 'col')
- d_denom: float32 [256, 20736], P('row', 'col')
- v_oovv: bfloat16 [256, 20736], P('row', 'col')
- v_vvvv: bfloat16 [20736, 20736], P('row', 'col')
- v_oooo: bfloat16 [256, 256], replicated
- w_ovov: bfloat16 [2304, 2304], P(None, 'col')
Outputs:
- output: float32 [2304, 2304], P('row', 'col')
All inputs are finite; a program needn't handle non-finite values.
Results may differ from a plain program's by a relative error of at most 0.001.
Values are sent between devices in bfloat16 or wider.
A program may use at most 1 GiB of HBM per device.

v0:
```python
import math
import jax
import jax.numpy as jnp
from jax import lax
from jax.sharding import PartitionSpec as P


def solution(mesh):
    row_n = mesh.shape["row"]
    col_n = mesh.shape["col"]

    def local_sweep(t_blk, d_blk, voovv_blk, vvvvv_blk, oooo_blk, wr_blk):
        n_occ = math.isqrt(oooo_blk.shape[0])
        n_vir = wr_blk.shape[0] // n_occ
        occ_r = n_occ // row_n
        occ_c = n_occ // col_n
        vir_c = n_vir // col_n
        t_bf = t_blk.astype(jnp.bfloat16)
        t_rows = lax.all_gather(t_bf, "col", axis=1, tiled=True)
        t_ladder = lax.all_to_all(t_rows, "row", 1, 0, tiled=True)
        ladder_part = jnp.dot(t_ladder, vvvvv_blk, preferred_element_type=jnp.float32)
        r_ladder = lax.psum_scatter(ladder_part, "row", scatter_dimension=0, tiled=True)
        t_cols = lax.all_gather(t_bf, "row", axis=0, tiled=True)
        x_part = lax.dot_general(voovv_blk, t_cols, (((1,), (1,)), ((), ())), preferred_element_type=jnp.float32)
        x_rows = lax.psum(x_part, "col")
        x_cols = lax.all_to_all(x_rows, "row", 1, 0, tiled=True)
        w_hole = (oooo_blk.astype(jnp.float32) + 0.5 * x_cols).astype(jnp.bfloat16)
        r_hole = lax.dot_general(w_hole, t_cols, (((0,), (0,)), ((), ())), preferred_element_type=jnp.float32)
        amp_four = t_rows.reshape(occ_r, n_occ, n_vir, n_vir)
        wr_three = wr_blk.reshape(n_occ, n_vir, occ_c * n_vir)
        r_mixed = jnp.einsum("ikac,kcn->ian", amp_four, wr_three, preferred_element_type=jnp.float32)
        r_mixed = r_mixed.reshape(occ_r, n_vir, occ_c, n_vir)
        mixed_entry = lax.all_to_all(r_mixed, "col", 1, 2, tiled=True)
        swap_rows = lax.all_to_all(mixed_entry, "row", 2, 0, tiled=True)
        swap_full = lax.all_to_all(swap_rows, "col", 3, 1, tiled=True)
        mixed_image = jnp.transpose(swap_full, (2, 3, 0, 1))
        base_sum = (voovv_blk.astype(jnp.float32) + r_ladder + r_hole).reshape(occ_r, n_occ, vir_c, n_vir)
        d_four = d_blk.reshape(occ_r, n_occ, vir_c, n_vir)
        total_sum = (jnp.transpose(base_sum, (0, 2, 1, 3)) + mixed_entry + mixed_image) / jnp.transpose(d_four, (0, 2, 1, 3))
        t_pairs = lax.all_to_all(total_sum, "col", 2, 1, tiled=True)
        return t_pairs.reshape(occ_r * n_vir, occ_c * n_vir)

    return jax.shard_map(
        local_sweep,
        mesh=mesh,
        in_specs=(P("row", "col"), P("row", "col"), P("row", "col"), P("row", "col"), P(None, "row"), P(None, "col")),
        out_specs=P("row", "col"),
        check_vma=False,
    )
```

profile of v0, /device:TPU:0, one launch (start us, length us, event | category | flops | bytes accessed | tf_op | source)
XLA Modules:
  0.0 372.1 jit_solution(17167845830243588040)
XLA Ops:
  6.5 0.0 copy-start
  6.5 0.0 all-gather.6.cloned.1.call-start
  6.5 2.3 convert_bitcast_fusion
  8.9 0.0 all-gather.6.cloned.1.call-update
  8.9 0.0 all-gather.4.cloned.1.call-start
  9.0 0.0 copy-done
  9.0 1.0 convert_element_type.13
  9.9 0.0 all-gather.4.cloned.1.call-update
  10.0 38.0 %all-gather.6.cloned.1.call-done = bf16[4,5184,64]{1,2,0:T(8,128)(2,1)} async-done(((bf16[1,5184,64]{1,2,0:T(8,128)(2,1)}), bf16[4,5184,64]{1,2,0:T(8,128)(2,1)}) %all-gather.6.cloned.1.call-update) | async-done | bytes 2654224 | tf_op jit(solution)/shard_map/all_gather | solution.py:19
  48.0 5.4 %copy.40 = bf16[4,5184,64]{1,0,2:T(4,128)(2,1)} copy(bf16[4,5184,64]{1,2,0:T(8,128)(2,1)} %all-gather.6.cloned.1.call-done) | data formatting | bytes 5308416 | tf_op jit(solution)/shard_map/all_gather | solution.py:19
  53.4 4.0 %reshape.42 = bf16[20736,64]{0,1:T(8,128)(2,1)S(1)} reshape(bf16[4,5184,64]{1,0,2:T(4,128)(2,1)} %copy.40) | data formatting | bytes 5308416
  57.4 4.2 %all_to_all.74 = bf16[64,4,5184]{2,1,0:T(4,128)(2,1)} reshape(bf16[64,20736]{1,0:T(8,128)(2,1)S(1)} %bitcast.74) | data formatting | bytes 5308416 | tf_op jit(solution)/shard_map/all_to_all | solution.py:20
  61.6 3.5 copy.41
  65.1 0.0 copy-start.1
  65.2 4.7 %all-to-all-start = ((bf16[64,4,5184]{2,0,1:T(8,128)(2,1)}), bf16[64,4,5184]{2,0,1:T(8,128)(2,1)}, u32[]{:S(2)}, u32[]{:S(2)}) async-start(bf16[64,4,5184]{2,0,1:T(8,128)(2,1)} %copy.41), calls=%async_computation | async-start | bytes 5373952 | tf_op jit(solution)/shard_map/all_to_all | solution.py:20
  69.9 0.0 all-reduce.2.cloned.1.call-start
  69.9 3.4 all-gather.4.cloned.1.call-done
  73.3 0.0 copy-done.1
  73.3 2.7 fusion.10
  76.0 0.1 all_to_all.78
  76.1 0.7 copy.42
  76.8 0.0 all-reduce.2.cloned.1.call-update
  76.8 0.3 reduce-scatter.2.cloned.1.call-start
  77.1 24.5 %all-to-all-done = bf16[64,4,5184]{2,0,1:T(8,128)(2,1)} async-done(((bf16[64,4,5184]{2,0,1:T(8,128)(2,1)}), bf16[64,4,5184]{2,0,1:T(8,128)(2,1)}, u32[]{:S(2)}, u32[]{:S(2)}) %all-to-all-start) | async-done | bytes 2654240 | tf_op jit(solution)/shard_map/all_to_all | solution.py:20
  101.6 25.9 %fusion.9 = f32[256,5184]{1,0:T(8,128)} fusion(bf16[256,5184]{1,0:T(8,128)(2,1)} %bitcast.4, bf16[5184,5184]{1,0:T(8,128)(2,1)} %param.9), kind=kOutput, calls=%fused_computation.12 | convolution fusion | flops 13759414272 | bytes 61710336 | tf_op jit(solution)/shard_map/dot_general | solution.py:21
  127.5 0.0 reduce-scatter.2.cloned.1.call-update
  127.5 4.5 %copy.43 = bf16[2304,576]{1,0:T(8,128)(2,1)} copy(bf16[2304,576]{0,1:T(8,128)(2,1)} %param.11) | data formatting | bytes 5308416 | tf_op args[5]
  132.0 10.2 %reshape.47 = bf16[4,144,144,16]{1,0,2,3:T(4,128)(2,1)} reshape(bf16[576,144,16]{0,1,2:T(8,128)(2,1)} %bitcast.81) | data formatting | bytes 5308416 | tf_op jit(solution)/shard_map/ikac,kcn->ian/dot_general | solution.py:31
  142.2 11.9 %copy.45 = bf16[4,144,144,16]{2,1,3,0:T(8,128)(2,1)} copy(bf16[4,144,144,16]{1,0,2,3:T(4,128)(2,1)} %reshape.47) | data formatting | bytes 5308416 | tf_op jit(solution)/shard_map/ikac,kcn->ian/dot_general | solution.py:31
  154.1 9.3 %reshape.43 = bf16[4,16,144,144,1]{3,2,1,0,4:T(8,128)(2,1)} reshape(bf16[64,20736]{1,0:T(8,128)(2,1)S(1)} %bitcast.75) | data formatting | bytes 5308416 | tf_op jit(solution)/shard_map/reshape | solution.py:29
  163.5 8.3 %fusion.3 = f32[4,144,4,144]{3,1,2,0:T(8,128)S(1)} fusion(bf16[4,144,144,16]{2,1,3,0:T(8,128)(2,1)} %copy.45, bf16[4,16,144,144,1]{3,2,1,0,4:T(8,128)(2,1)} %reshape.43), kind=kOutput, calls=%fused_computation.8 | convolution fusion | flops 1528823808 | bytes 6635520 | tf_op jit(solution)/shard_map/ikac,kcn->ian/dot_general | solution.py:31
  171.8 1.5 copy.46
  173.3 31.3 %all_to_all.101 = f32[4,144,4,144]{3,2,0,1:T(4,128)S(1)} all-to-all(f32[4,144,4,144]{3,2,0,1:T(4,128)S(1)} %copy.46), channel_id=1, replica_groups=mesh['col'=4,'row'=4] {'col'}, dimensions={1} | all-to-all | bytes 2654208 | tf_op jit(solution)/shard_map/all_to_all | solution.py:33
  204.6 1.4 copy.48
  206.0 3.0 copy.49
  209.0 4.5 %all-to-all-start.3 = ((f32[4,36,16,144]{3,0,1,2:T(4,128)}), f32[4,36,16,144]{3,0,1,2:T(4,128)}, u32[]{:S(2)}, u32[]{:S(2)}) async-start(f32[4,36,16,144]{3,0,1,2:T(4,128)} %copy.49), calls=%async_computation.4 | async-start | bytes 4718592 | tf_op jit(solution)/shard_map/all_to_all | solution.py:34
  213.5 0.0 all-reduce.2.cloned.1.call-done
  213.5 1.6 reshape.48
  215.2 26.5 %all-to-all-done.3 = f32[4,36,16,144]{3,0,1,2:T(4,128)} async-done(((f32[4,36,16,144]{3,0,1,2:T(4,128)}), f32[4,36,16,144]{3,0,1,2:T(4,128)}, u32[]{:S(2)}, u32[]{:S(2)}) %all-to-all-start.3) | async-done | bytes 1327136 | tf_op jit(solution)/shard_map/all_to_all | solution.py:34
  241.7 3.3 all-to-all-start.1
  245.0 4.6 %copy.50 = f32[4,36,4,4,144]{4,3,1,0,2:T(4,128)} copy(f32[4,36,4,4,144]{4,0,1,3,2:T(4,128)} %bitcast.19) | data formatting | bytes 2654208 | tf_op jit(solution)/shard_map/all_to_all | solution.py:34
  249.6 7.9 %copy.51 = f32[16,36,4,144]{1,0,2,3:T(8,128)} copy(f32[16,36,4,144]{3,2,1,0:T(4,128)} %bitcast.82) | data formatting | bytes 2654208 | tf_op jit(solution)/shard_map/all_to_all | solution.py:34
  257.5 7.6 %reshape.50 = f32[4,1,82944]{2,1,0:T(1,128)} reshape(f32[144,4,16,36]{3,2,1,0:T(8,128)} %bitcast.78) | data formatting | bytes 2654208
  265.1 0.0 all-to-all-done.1
  265.1 4.6 %all-to-all-start.4 = ((f32[4,1,82944]{2,1,0:T(1,128)}), f32[4,1,82944]{2,1,0:T(1,128)}, u32[]{:S(2)}, u32[]{:S(2)}) async-start(f32[4,1,82944]{2,1,0:T(1,128)} %reshape.50), calls=%async_computation.5 | async-start | bytes 2654208 | tf_op jit(solution)/shard_map/all_to_all | solution.py:35
  269.7 0.0 copy-done.2
  269.7 0.6 dynamic-slice
  271.0 3.7 reshape.31
  274.7 0.5 broadcast.5
  275.2 0.8 reduce
  276.0 0.1 reshape.49
  276.2 0.9 fusion.8
  277.1 9.8 %all-to-all-done.4 = f32[4,1,82944]{2,1,0:T(1,128)} async-done(((f32[4,1,82944]{2,1,0:T(1,128)}), f32[4,1,82944]{2,1,0:T(1,128)}, u32[]{:S(2)}, u32[]{:S(2)}) %all-to-all-start.4) | async-done | bytes 1327136 | tf_op jit(solution)/shard_map/all_to_all | solution.py:35
  286.9 6.5 %reduce.1 = f32[4,82944]{1,0:T(4,128)} reduce(f32[4,1,82944]{2,1,0:T(1,128)} %all-to-all-done.4, f32[]{:T(128)} %broadcast.5), dimensions={1}, to_apply=%all_to_all.88.reduce_sub_computation | reduce | bytes 2654212 | tf_op jit(solution)/shard_map/all_to_all | solution.py:35
  293.4 9.8 %reshape.51 = f32[144,4,16,36]{3,2,1,0:T(8,128)} reshape(f32[4,82944]{1,0:T(4,128)} %reduce.1) | data formatting | bytes 2654208
  303.2 7.6 %copy.66 = f32[16,36,4,4,36]{1,3,0,4,2:T(4,128)} copy(f32[16,36,4,4,36]{1,0,2,4,3:T(8,128)} %bitcast.79) | data formatting | bytes 2654208 | tf_op jit(solution)/shard_map/all_to_all | solution.py:35
  310.7 5.4 %all_to_all.91 = f32[16,144,4,36]{1,0,3,2:T(8,128)} reshape(f32[16,4,36,4,36]{2,1,0,4,3:T(4,128)} %bitcast.80) | data formatting | bytes 2654208 | tf_op jit(solution)/shard_map/all_to_all | solution.py:35
  316.2 3.8 %convolution_add_fusion = f32[64,5184]{1,0:T(8,128)} fusion(bf16[256,64]{1,0:T(8,128)(2,1)S(1)} %fusion.8, bf16[256,5184]{1,0:T(8,128)(2,1)} %all-gather.4.cloned.1.call-done, f32[64,5184]{1,0:T(8,128)} %reduce-scatter.2.cloned.1.call-done, bf16[64,5184]{1,0:T(8,128)(2,1)S(1)} %copy-done.1), kind=kOutput, calls=%fused_computation | convolution fusion | flops 170864640 | bytes 6004736 | tf_op jit(solution)/shard_map/dot_general | solution.py:28
  320.0 3.7 reshape.28
  323.6 5.1 %bitcast_divide_fusion = f32[4,36,16,144]{3,1,2,0:T(8,128)S(1)} fusion(f32[4,16,36,144]{3,2,1,0:T(8,128)} %reshape.31, f32[4,36,16,144]{3,1,2,0:T(8,128)S(1)} %bitcast.77, f32[4,16,36,144]{3,2,1,0:T(8,128)} %reshape.28, f32[16,144,4,36]{1,0,3,2:T(8,128)} %all_to_all.91), kind=kLoop, calls=%fused_computation.5 | loop fusion | flops 995328 | bytes 6635520 | tf_op jit(solution)/shard_map/div | solution.py:39
  328.7 1.5 copy.55
  330.3 30.8 %all_to_all.102 = f32[4,36,16,144]{3,0,1,2:T(4,128)S(1)} all-to-all(f32[4,36,16,144]{3,0,1,2:T(4,128)S(1)} %copy.55), channel_id=1, replica_groups=mesh['col'=4,'row'=4] {'col'}, dimensions={2} | all-to-all | bytes 2654208 | tf_op jit(solution)/shard_map/all_to_all | solution.py:40
  361.1 1.5 copy.56
  362.6 2.8 reshape.32
  (3 shorter events, 0.0 us)
Async XLA Ops:
  6.5 2.4 copy-start
  6.5 41.5 %all-gather.6.cloned.1.call-start = ((), (), s32[]{:S(2)}) async-start(), calls=%async_computation.10 | async-start | bytes 3358720 | tf_op jit(solution)/shard_map/all_gather | solution.py:19
  8.9 64.4 %all-gather.4.cloned.1.call-start = ((), (), s32[]{:S(2)}) async-start(), calls=%async_computation.8 | async-start | bytes 3358720 | tf_op jit(solution)/shard_map/all_gather | solution.py:23
  65.1 8.1 %copy-start.1 = (bf16[64,5184]{1,0:T(8,128)(2,1)S(1)}, bf16[64,5184]{1,0:T(8,128)(2,1)}, u32[]{:S(2)}) copy-start(bf16[64,5184]{1,0:T(8,128)(2,1)} %param.8) | copy-start | bytes 1990660
  65.2 36.5 %all-to-all-start = ((bf16[64,4,5184]{2,0,1:T(8,128)(2,1)}), bf16[64,4,5184]{2,0,1:T(8,128)(2,1)}, u32[]{:S(2)}, u32[]{:S(2)}) async-start(bf16[64,4,5184]{2,0,1:T(8,128)(2,1)} %copy.41), calls=%async_computation | async-start | bytes 5373952 | tf_op jit(solution)/shard_map/all_to_all | solution.py:20
  69.9 143.7 %all-reduce.2.cloned.1.call-start = ((), (), s32[]{:S(2)}) async-start(), calls=%async_computation.9 | async-start | bytes 262144 | tf_op jit(solution)/shard_map/psum | solution.py:25
  76.8 239.4 %reduce-scatter.2.cloned.1.call-start = ((), (), s32[]{:S(2)}) async-start(), calls=%async_computation.7 | async-start | bytes 6717440 | tf_op jit(solution)/shard_map/reduce_scatter | solution.py:22
  209.0 32.7 %all-to-all-start.3 = ((f32[4,36,16,144]{3,0,1,2:T(4,128)}), f32[4,36,16,144]{3,0,1,2:T(4,128)}, u32[]{:S(2)}, u32[]{:S(2)}) async-start(f32[4,36,16,144]{3,0,1,2:T(4,128)} %copy.49), calls=%async_computation.4 | async-start | bytes 4718592 | tf_op jit(solution)/shard_map/all_to_all | solution.py:34
  241.7 23.4 %all-to-all-start.1 = ((f32[4,1,4096]{2,1,0:T(1,128)}), f32[4,1,4096]{2,1,0:T(1,128)S(1)}, u32[]{:S(2)}, u32[]{:S(2)}) async-start(f32[4,1,4096]{2,1,0:T(1,128)} %reshape.48), calls=%async_computation.2 | async-start | bytes 131072 | tf_op jit(solution)/shard_map/all_to_all | solution.py:26
  265.1 4.6 %copy-start.2 = (u32[16]{0:T(128)S(1)}, u32[16]{0:T(128)}, u32[]{:S(2)}) copy-start(u32[16]{0:T(128)} %constant.2) | copy-start | bytes 196
  265.1 21.8 %all-to-all-start.4 = ((f32[4,1,82944]{2,1,0:T(1,128)}), f32[4,1,82944]{2,1,0:T(1,128)}, u32[]{:S(2)}, u32[]{:S(2)}) async-start(f32[4,1,82944]{2,1,0:T(1,128)} %reshape.50), calls=%async_computation.5 | async-start | bytes 2654208 | tf_op jit(solution)/shard_map/all_to_all | solution.py:35
Sparse Core Ops, SparseCore 0:
  9.1 38.8 all-gather.5
  49.5 23.6 all-gather.3
  76.9 34.5 all-reduce.1
  127.6 46.4 reduce-scatter.1
where the time goes:
time: 378 us; the launch traced here: 372 us
  local copies, waits for them, and re-layouts  119 us (31%)
  waiting for transfers between devices  102 us (27%)
  blocking collectives  62.1 us (16%)
  matrix products  40.7 us (11%)
  starting transfers between devices  17.5 us (5%)
  other arithmetic  16.6 us (4%)
  between operations  14.2 us (4%)
    all_gather x1, waiting for transfers between devices, local_sweep(): t_rows = lax.all_gather(t_bf, 'col', axis=1, tiled=True)  38 us
    all_to_all x1, blocking collectives, local_sweep(): mixed_entry = lax.all_to_all(r_mixed, 'col', 1, 2, tiled=True)  31.3 us
    all_to_all x1, blocking collectives, local_sweep(): t_pairs = lax.all_to_all(total_sum, 'col', 2, 1, tiled=True)  30.8 us
    unnamed x12, local copies, waits for them, and re-layouts  27.7 us
    all_to_all x1, waiting for transfers between devices, local_sweep(): swap_rows = lax.all_to_all(mixed_entry, 'row', 2, 0, tiled=True)  26.5 us
    dot_general x1, matrix products, local_sweep(): jnp.dot(t_ladder, vvvvv_blk, preferred_element_type=jnp.float32)  25.9 us
    all_to_all x1, waiting for transfers between devices, local_sweep(): t_ladder = lax.all_to_all(t_rows, 'row', 1, 0, tiled=True)  24.5 us
    dot_general x3, local copies, waits for them, and re-layouts, local_sweep(): jnp.einsum('ikac,kcn->ian', amp_four, wr_three, preferred_element_type=jn...  23.6 us
  transfers between devices with their start and end apart: 8, of which 5 were waited for; matrix products, arithmetic and copies ran while one was open for 39% of the time, Pallas kernels for 0%

commit v1 on v0

v1 whole, which is shorter than its diff:
```python
import functools

import jax
import jax.numpy as jnp
from jax import lax
from jax.experimental import pallas as pl
from jax.experimental.pallas import tpu as pltpu
from jax.sharding import PartitionSpec as P

MESH = pl.DeviceIdType.MESH
F32 = jnp.float32
BF16 = jnp.bfloat16

O = 16
V = 144
RB = 64
CB = 5184
AB = 36
PB = 576
CW = 512
NCH = CB // CW
TW = CB - NCH * CW


def split_cols(load, planes, m):
    for q in range(8 if m < 4 else 4):
        piece = load(m, q)
        base = RB * (8 * m + q)
        planes[0, base : base + RB, :] = piece[:, 0:128]
        planes[1, base : base + RB, 0:16] = piece[:, 128:144]


def take_j(planes, j, base, rows):
    wide = planes[0, pl.ds(base + j, rows, stride=16), :]
    rest = planes[1, pl.ds(base + j, rows, stride=16), :]
    return [wide, rest[:, 0:16]]


def kernel(
    t_hbm, d_hbm, vo_hbm, vv_hbm, oo_ref, w_hbm, out_ref,
    t32, d32, vo, wv, trow, tcol, tlad, planes, tm, r3, pp, pt, pr,
    dsnd, drcv, lsnd, lrcv, planes2, xq, xqr, wt, vbuf, vtail,
    acc, d2r, xsb, xrb, acct, d2t, xst, xrt, r1,
    in_sem, v_sem, row_s, row_r, col_s, col_r, lad_s, lad_r, q_s, q_r,
    d_s, d_r, l_s, l_r, p_s, p_r, dd_s, dd_r, xx_s, xx_r,
):
    r = lax.axis_index("row")
    c = lax.axis_index("col")
    x, k = r // 2, r % 2
    z, y = c // 2, c % 2
    r_k, r_x = 2 * x + 1 - k, 2 * (1 - x) + k
    r_d = 2 * (1 - x) + 1 - k
    c_y, c_z = 2 * z + 1 - y, 2 * (1 - z) + y
    c_d = 2 * (1 - z) + 1 - y
    col_peers = (c_y, c_z, c_d)

    def send(src, dst, ss, rs, row, col):
        return pltpu.make_async_remote_copy(
            src_ref=src, dst_ref=dst, send_sem=ss, recv_sem=rs,
            device_id={"row": row, "col": col}, device_id_type=MESH,
        )

    def load_v(n, slot):
        at = pl.multiple_of(n * CW, CW)
        return pltpu.make_async_copy(vv_hbm.at[:, pl.ds(at, CW)], vbuf.at[slot], v_sem.at[slot])

    load_t = pltpu.make_async_copy(t_hbm, t32, in_sem.at[0])
    load_d = pltpu.make_async_copy(d_hbm, d32, in_sem.at[1])
    load_vo = pltpu.make_async_copy(vo_hbm, vo, in_sem.at[2])
    load_w = pltpu.make_async_copy(w_hbm, wv, in_sem.at[3])
    load_tail = pltpu.make_async_copy(vv_hbm.at[:, pl.ds(NCH * CW, TW)], vtail, in_sem.at[4])
    load_t.start()
    load_w.start()
    load_d.start()
    load_vo.start()
    load_tail.start()
    load_v(0, 0).start()
    load_v(1, 1).start()

    barrier = pltpu.get_barrier_semaphore()
    for rr in range(4):
        for cc in range(4):
            pl.semaphore_signal(barrier, inc=1, device_id={"row": rr, "col": cc}, device_id_type=MESH)

    load_t.wait()
    for m in range(9):
        piece = t32[:, PB * m : PB * m + PB].astype(BF16)
        trow[c, :, PB * m : PB * m + PB] = piece
        tcol[r, :, PB * m : PB * m + PB] = piece
    pl.semaphore_wait(barrier, 16)

    half = RB // 2
    row_copy = (
        send(trow.at[c], trow.at[c], row_s.at[0], row_r.at[0], r, c_y),
        send(trow.at[c], trow.at[c], row_s.at[1], row_r.at[1], r, c_z),
        send(trow.at[c_z, 0:half], trow.at[c_z, 0:half], row_s.at[2], row_r.at[2], r, c_y),
        send(trow.at[c_y, half:RB], trow.at[c_y, half:RB], row_s.at[3], row_r.at[3], r, c_z),
    )
    row_land = (
        send(trow.at[c_y], trow.at[c_y], row_s.at[0], row_r.at[0], r, c_y),
        send(trow.at[c_z], trow.at[c_z], row_s.at[1], row_r.at[1], r, c_z),
        send(trow.at[c_d, 0:half], trow.at[c_d, 0:half], row_s.at[2], row_r.at[2], r, c_y),
        send(trow.at[c_d, half:RB], trow.at[c_d, half:RB], row_s.at[3], row_r.at[3], r, c_z),
    )
    col_copy = (
        send(tcol.at[r], tcol.at[r], col_s.at[0], col_r.at[0], r_x, c),
        send(tcol.at[r], tcol.at[r], col_s.at[1], col_r.at[1], r_k, c),
        send(tcol.at[r_x], tcol.at[r_x], col_s.at[2], col_r.at[2], r_k, c),
    )
    col_land = (
        send(tcol.at[r_x], tcol.at[r_x], col_s.at[0], col_r.at[0], r_x, c),
        send(tcol.at[r_k], tcol.at[r_k], col_s.at[1], col_r.at[1], r_k, c),
        send(tcol.at[r_d], tcol.at[r_d], col_s.at[2], col_r.at[2], r_k, c),
    )
    row_copy[0].start()
    row_copy[1].start()
    col_copy[0].start()
    col_copy[1].start()

    def lad_copy(slot):
        return send(trow.at[slot], tlad.at[r], lad_s.at[slot], lad_r.at[r], slot, c)

    def dispatch(slot):
        @pl.when(slot != r)
        def _():
            lad_copy(slot).start()

        @pl.when(slot == r)
        def _():
            tlad[r] = trow[slot]

    dispatch(c)

    def bf16_piece(slot):
        def load(m, q):
            width = 1152 if m < 4 else 576
            stripe = trow[slot, :, 1152 * m : 1152 * m + width].astype(F32)
            return stripe[:, V * q : V * q + V]

        return load

    load_w.wait()

    def mixed(slot):
        load = bf16_piece(slot)
        for m in range(5):
            split_cols(load, planes, m)
        for h in range(2):
            parts = []
            for j in range(8):
                parts += take_j(planes, 8 * h + j, 0, 4 * AB)
            tm[:, 1152 * h : 1152 * h + 1152] = jnp.concatenate(parts, axis=1).astype(BF16)
        at = pl.multiple_of(slot * V, 8)
        r3[pl.ds(at, V), :] = jnp.dot(tm[...], wv[...], preferred_element_type=F32)

    mixed(c)

    load_d.wait()
    for m in range(5):
        split_cols(lambda m, q: d32[:, 1152 * m + V * q : 1152 * m + V * q + V], planes, m)
    for cc in range(4):
        parts = []
        for j in range(4):
            parts += take_j(planes, 4 * cc + j, 0, 4 * AB)
        dsnd[cc] = jnp.concatenate(parts, axis=1)
    own_rows = pl.ds(pl.multiple_of(c * V, 8), V)
    drcv[own_rows, :] = dsnd[c]

    row_land[1].wait_recv()
    row_copy[2].start()
    dispatch(c_z)
    row_land[0].wait_recv()
    row_copy[3].start()
    dispatch(c_y)
    mixed(c_z)
    mixed(c_y)

    col_land[0].wait_recv()
    col_copy[2].start()

    row_land[2].wait_recv()
    row_land[3].wait_recv()
    dispatch(c_d)
    d_copy = [
        send(dsnd.at[peer], drcv.at[own_rows], d_s.at[q], d_r.at[q], r, peer) for q, peer in enumerate(col_peers)
    ]
    for copy in d_copy:
        copy.start()
    mixed(c_d)

    for b in range(5):
        n = 128 if b < 4 else 64
        planes2[b, :, 0:n] = r3[:, 128 * b : 128 * b + n]
        for i in range(4):
            pp[V * i : V * i + V, 128 * b : 128 * b + n] = planes2[b, pl.ds(i, V, stride=4), :][:, 0:n]
    pt[...] = pp[...].T

    load_vo.wait()
    col_land[1].wait_recv()
    col_land[2].wait_recv()
    xq[...] = lax.dot_general(
        vo[...], tcol[...].reshape(4 * RB, CB), (((1,), (1,)), ((), ())), preferred_element_type=F32
    )
    xqr[c] = xq[...]
    q_copy = [send(xq, xqr.at[c], q_s.at[q], q_r.at[q], r, peer) for q, peer in enumerate(col_peers)]
    for copy in q_copy:
        copy.start()

    p_copy = send(pt, pr, p_s.at[0], p_r.at[0], c, r)

    @pl.when(r != c)
    def _():
        p_copy.start()

    @pl.when(r == c)
    def _():
        pr[...] = pt[...]

    for q, peer in enumerate(col_peers):
        send(xq, xqr.at[peer], q_s.at[q], q_r.at[q], r, peer).wait_recv()
    x_sum = (xqr[0] + xqr[1]) + (xqr[2] + xqr[3])
    w_hole = oo_ref[...].astype(F32) + 0.5 * x_sum
    wt[...] = w_hole.T.astype(BF16)

    for rr in range(4):

        @pl.when(r != rr)
        def _():
            send(trow.at[0], tlad.at[rr], lad_s.at[rr], lad_r.at[rr], rr, c).wait_recv()

    def d2_copy(n):
        return send(acc.at[n, 1 - k], d2r.at[n], dd_s.at[n], dd_r.at[n], r_k, c)

    def xx_copy(n):
        return send(xsb.at[n], xrb.at[n], xx_s.at[n], xx_r.at[n], r_x, c)

    d2_tail = send(acct.at[1 - k], d2t, dd_s.at[NCH], dd_r.at[NCH], r_k, c)
    xx_tail = send(xst, xrt, xx_s.at[NCH], xx_r.at[NCH], r_x, c)

    load_tail.wait()
    part = jnp.dot(tlad[...].reshape(4 * RB, CB), vtail[...], preferred_element_type=F32)
    part = part + jnp.dot(wt[...], trow[c, :, NCH * CW : CB], preferred_element_type=F32)
    for rr in range(4):
        acct[rr % 2, rr // 2] = part[RB * rr : RB * rr + RB]
    d2_tail.start()

    def second(n):
        d2_copy(n).wait_recv()
        xsb[n] = acc[n, k, 1 - x] + d2r[n, 1 - x]
        at = pl.multiple_of(n * CW, CW)
        r1[:, pl.ds(at, CW)] = acc[n, k, x] + d2r[n, x]
        xx_copy(n).start()

    def ladder_step(n, carry):
        slot = n % 2
        load_v(n, slot).wait()
        at = pl.multiple_of(n * CW, CW)
        for h in range(2):
            part = jnp.dot(
                tlad[...].reshape(4 * RB, CB), vbuf[slot, :, 256 * h : 256 * h + 256], preferred_element_type=F32
            )
            part = part + jnp.dot(
                wt[...], trow[c, :, pl.ds(pl.multiple_of(at + 256 * h, 256), 256)], preferred_element_type=F32
            )
            for rr in range(4):
                acc[n, rr % 2, rr // 2, :, 256 * h : 256 * h + 256] = part[RB * rr : RB * rr + RB]
        d2_copy(n).start()

        @pl.when(n + 2 < NCH)
        def _():
            load_v(n + 2, slot).start()

        @pl.when(n == 0)
        def _():
            d2_tail.wait_recv()
            xst[...] = acct[k, 1 - x] + d2t[1 - x]
            r1[:, NCH * CW : CB] = acct[k, x] + d2t[x]
            xx_tail.start()

        @pl.when(n > 0)
        def _():
            second(n - 1)

        return carry

    lax.fori_loop(0, NCH, ladder_step, 0)
    second(NCH - 1)

    l_copy = []
    xx_tail.wait_recv()
    r1[:, NCH * CW : CB] += xrt[...] + vo[:, NCH * CW : CB].astype(F32)
    done = 0
    for m in range(5):
        width = 1152 if m < 4 else 576
        while done < NCH and CW * done < 1152 * m + width:
            xx_copy(done).wait_recv()
            at = CW * done
            r1[:, at : at + CW] += xrb[done] + vo[:, at : at + CW].astype(F32)
            done += 1
        split_cols(lambda m, q: r1[:, 1152 * m + V * q : 1152 * m + V * q + V], planes, m)
        rows = width // V * 4
        first = 32 * m
        for cc in range(4):
            parts = []
            for j in range(4):
                parts += take_j(planes, 4 * cc + j, RB * 8 * m, rows)
            lsnd[cc, first : first + rows, :] = jnp.concatenate(parts, axis=1)
        there = pl.ds(pl.multiple_of(c * V + first, 8), rows)
        lrcv[there, :] = lsnd[c, first : first + rows, :]
        for q, peer in enumerate(col_peers):
            copy = send(
                lsnd.at[peer, first : first + rows], lrcv.at[there], l_s.at[m, q], l_r.at[m, q], r, peer
            )
            copy.start()
            l_copy.append(copy)

    @pl.when(r != c)
    def _():
        p_copy.wait_recv()

    pp[...] = pp[...] + pr[...]
    for q, peer in enumerate(col_peers):
        at = pl.ds(pl.multiple_of(peer * V, 8), V)
        send(dsnd.at[peer], drcv.at[at], d_s.at[q], d_r.at[q], r, peer).wait_recv()
    for m in range(5):
        rows = 32 if m < 4 else 16
        for q, peer in enumerate(col_peers):
            at = pl.ds(pl.multiple_of(peer * V + 32 * m, 8), rows)
            send(
                lsnd.at[peer, 32 * m : 32 * m + rows], lrcv.at[at], l_s.at[m, q], l_r.at[m, q], r, peer
            ).wait_recv()
    for b in range(5):
        n = 128 if b < 4 else 64
        cols = slice(128 * b, 128 * b + n)
        planes[0, 0:PB, 0:n] = lrcv[:, cols]
        planes2[b, :, 0:n] = drcv[:, cols]
        for i in range(4):
            rows = slice(V * i, V * i + V)
            top = planes[0, pl.ds(i, V, stride=4), :][:, 0:n] + pp[rows, cols]
            out_ref[rows, cols] = top / planes2[b, pl.ds(i, V, stride=4), :][:, 0:n]

    for copy in (*row_copy, *col_copy, *q_copy, *d_copy, *l_copy, d2_tail, xx_tail):
        copy.wait_send()
    for slot in range(4):

        @pl.when(slot != r)
        def _():
            lad_copy(slot).wait_send()

    @pl.when(r != c)
    def _():
        p_copy.wait_send()

    def drain(n, carry):
        d2_copy(n).wait_send()
        xx_copy(n).wait_send()
        return carry

    lax.fori_loop(0, NCH, drain, 0)


def solution(mesh):
    vm = pltpu.VMEM
    dma = pltpu.SemaphoreType.DMA
    scratch = [
        vm((RB, CB), F32), vm((RB, CB), F32), vm((RB, CB), BF16), vm((O * V, PB), BF16),
        vm((4, RB, CB), BF16), vm((4, RB, CB), BF16), vm((4, RB, CB), BF16),
        vm((2, AB * RB, 128), F32), vm((V, O * V), BF16),
        vm((PB, PB), F32), vm((PB, PB), F32), vm((PB, PB), F32), vm((PB, PB), F32),
        vm((4, V, PB), F32), vm((PB, PB), F32), vm((4, V, PB), F32), vm((PB, PB), F32),
        vm((5, PB, 128), F32),
        vm((RB, O * O), F32), vm((4, RB, O * O), F32), vm((O * O, RB), BF16),
        vm((2, CB, CW), BF16), vm((CB, TW), BF16),
        vm((NCH, 2, 2, RB, CW), F32), vm((NCH, 2, RB, CW), F32), vm((NCH, RB, CW), F32), vm((NCH, RB, CW), F32),
        vm((2, 2, RB, TW), F32), vm((2, RB, TW), F32), vm((RB, TW), F32), vm((RB, TW), F32),
        vm((RB, CB), F32),
        dma((5,)), dma((2,)), dma((4,)), dma((4,)), dma((3,)), dma((3,)), dma((4,)), dma((4,)), dma((3,)), dma((3,)),
        dma((3,)), dma((3,)), dma((5, 3)), dma((5, 3)), dma((1,)), dma((1,)),
        dma((NCH + 1,)), dma((NCH + 1,)), dma((NCH + 1,)), dma((NCH + 1,)),
    ]
    hbm = pl.BlockSpec(memory_space=pl.ANY)
    vmem = pl.BlockSpec(memory_space=pltpu.VMEM)
    call = pl.pallas_call(
        kernel,
        out_shape=jax.ShapeDtypeStruct((PB, PB), F32),
        in_specs=[hbm, hbm, hbm, hbm, vmem, hbm],
        out_specs=vmem,
        scratch_shapes=scratch,
        compiler_params=pltpu.CompilerParams(
            collective_id=0, has_side_effects=True, vmem_limit_bytes=67_000_000
        ),
        name="sweep",
    )
    return jax.shard_map(
        call,
        mesh=mesh,
        in_specs=(P("row", "col"), P("row", "col"), P("row", "col"), P("row", "col"), P("row", None), P(None, "col")),
        out_specs=P("row", "col"),
        check_vma=False,
    )
```

time: 378 us -> 129 us (0.34); the launches traced: 372 us -> 128 us
  Pallas kernels: 0 us -> 118 us
  local copies, waits for them, and re-layouts: 119 us -> 9.7 us
  waiting for transfers between devices: 102 us -> 0 us
  blocking collectives: 62.1 us -> 0 us
  matrix products: 40.7 us -> 0 us
  starting transfers between devices: 17.5 us -> 0 us
  other arithmetic: 16.6 us -> 0 us
  between operations: 14.2 us -> 0.66 us
    pallas_call x0 -> x1, Pallas kernels: none -> 118 us
    all_to_all x2 -> x0, blocking collectives: 62.1 us -> none  [the longest x1 31.3 us: local_sweep(): mixed_entry = lax.all_to_all(r_mixed, 'col', 1, 2, tiled=True)]
    all_to_all x4 -> x0, waiting for transfers between devices: 60.9 us -> none  [the longest x1 26.5 us: local_sweep(): swap_rows = lax.all_to_all(mixed_entry, 'row', 2, 0, tiled=True)]
    all_gather x2 -> x0, waiting for transfers between devices: 41.4 us -> none  [the longest x1 38 us: local_sweep(): t_rows = lax.all_gather(t_bf, 'col', axis=1, tiled=True)]
    dot_general x4 -> x0, matrix products: 40.7 us -> none  [the longest x1 25.9 us: local_sweep(): jnp.dot(t_ladder, vvvvv_blk, preferred_element_type=jnp.float32)]
    all_to_all x12 -> x0, local copies, waits for them, and re-layouts: 40.5 us -> none  [the longest x2 13 us: local_sweep(): swap_full = lax.all_to_all(swap_rows, 'col', 3, 1, tiled=True)]
    dot_general x3 -> x0, local copies, waits for them, and re-layouts: 23.6 us -> none  [local_sweep(): jnp.einsum('ikac,kcn->ian', amp_four, wr_three, preferred_element_type=jn...]
    unnamed x12 -> x2, local copies, waits for them, and re-layouts: 27.7 us -> 7.08 us
  transfers between devices with their start and end apart: 8 -> 0, of which waited for: 5 -> 0; matrix products, arithmetic and copies ran while one was open for 39% -> 0% of each run, Pallas kernels for 0% -> 0%
where the time goes in v1:
time: 129 us; the launch traced here: 128 us
  Pallas kernels  118 us (91%)
  local copies, waits for them, and re-layouts  9.7 us (8%)
    pallas_call x1, Pallas kernels  118 us
    unnamed x2, local copies, waits for them, and re-layouts  7.08 us
    another operation x2, local copies, waits for them, and re-layouts  2.62 us

profile of v1, /device:TPU:0, one launch (start us, length us, event | category | flops | bytes accessed | tf_op | source)
XLA Modules:
  0.0 128.3 jit_solution(2895423930958681920)
XLA Ops:
  0.0 1.2 dynamic-slice
  1.9 1.4 %constant_dynamic-slice_fusion.oo_ref = bf16[64,256]{1,0:T(8,128)(2,1)} fusion(bf16[256,256]{1,0:T(8,128)(2,1)} %param.10, s32[]{:T(128)} %bitcast), kind=kLoop, calls=%fused_computation | loop fusion | bytes 65540 | tf_op jit(solution)/call_exported
  3.3 4.5 %copy.7.w_hbm = bf16[2304,576]{1,0:T(8,128)(2,1)} copy(bf16[2304,576]{0,1:T(8,128)(2,1)} %param.11) | data formatting | bytes 5308416 | tf_op args[5]
  7.8 117.9 %sweep.1 = f32[576,576]{1,0:T(8,128)} custom-call(f32[64,5184]{1,0:T(8,128)} %t_hbm.1, f32[64,5184]{1,0:T(8,128)} %d_hbm.1, bf16[64,5184]{1,0:T(8,128)(2,1)} %vo_hbm.1, bf16[5184,5184]{1,0:T(8,128)(2,1)} %vv_hbm.1, bf16[64,256]{1,0:T(8,128)(2,1)} %constant_dynamic-slice_fusion.oo_ref, bf16[2304,576]{1,0:T(8,128)(2,1)} %copy.7.w_hbm), custom_call_target="tpu_custom_call" | custom-call | tf_op jit(solution)/shard_map/sweep/pallas_call
  125.7 2.6 %copy.9 = f32[576,576]{1,0:T(8,128)} copy(f32[576,576]{1,0:T(8,128)} %sweep.1) | data formatting | bytes 2654208

commit v2 on v1

--- a/solution.py
+++ b/solution.py
@@ -22,9 +22,16 @@
 TW = CB - NCH * CW
 
 
+def stripe(load, m, q):
+    first = 1152 * m + V * q
+    low = first // 128 * 128
+    high = min(-(-(first + V) // 128) * 128, CB)
+    return load(low, high)[:, first - low : first - low + V]
+
+
 def split_cols(load, planes, m):
     for q in range(8 if m < 4 else 4):
-        piece = load(m, q)
+        piece = stripe(load, m, q)
         base = RB * (8 * m + q)
         planes[0, base : base + RB, :] = piece[:, 0:128]
         planes[1, base : base + RB, 0:16] = piece[:, 128:144]
@@ -37,12 +44,12 @@
 
 
 def kernel(
-    t_hbm, d_hbm, vo_hbm, vv_hbm, oo_ref, w_hbm, out_ref,
+    t_hbm, d_hbm, vo_hbm, vv_hbm, oo_hbm, w_hbm, out_ref,
     t32, d32, vo, wv, trow, tcol, tlad, planes, tm, r3, pp, pt, pr,
-    dsnd, drcv, lsnd, lrcv, planes2, xq, xqr, wt, vbuf, vtail,
+    dsnd, drcv, lsnd, lrcv, planes2, xq, xqr, wt, oo, wblk, wf, vbuf, vtail,
     acc, d2r, xsb, xrb, acct, d2t, xst, xrt, r1,
     in_sem, v_sem, row_s, row_r, col_s, col_r, lad_s, lad_r, q_s, q_r,
-    d_s, d_r, l_s, l_r, p_s, p_r, dd_s, dd_r, xx_s, xx_r,
+    d_s, d_r, l_s, l_r, p_s, p_r, dd_s, dd_r, xx_s, xx_r, w_s, w_r, f_s,
 ):
     r = lax.axis_index("row")
     c = lax.axis_index("col")
@@ -69,11 +76,13 @@
     load_vo = pltpu.make_async_copy(vo_hbm, vo, in_sem.at[2])
     load_w = pltpu.make_async_copy(w_hbm, wv, in_sem.at[3])
     load_tail = pltpu.make_async_copy(vv_hbm.at[:, pl.ds(NCH * CW, TW)], vtail, in_sem.at[4])
+    load_oo = pltpu.make_async_copy(oo_hbm.at[pl.ds(pl.multiple_of(r * RB, RB), RB)], oo, in_sem.at[5])
     load_t.start()
     load_w.start()
     load_d.start()
     load_vo.start()
     load_tail.start()
+    load_oo.start()
     load_v(0, 0).start()
     load_v(1, 1).start()
 
@@ -114,7 +123,11 @@
     )
     row_copy[0].start()
     row_copy[1].start()
-    col_copy[0].start()
+
+    @pl.when(x == z)
+    def _():
+        col_copy[0].start()
+
     col_copy[1].start()
 
     def lad_copy(slot):
@@ -131,33 +144,26 @@
 
     dispatch(c)
 
-    def bf16_piece(slot):
-        def load(m, q):
-            width = 1152 if m < 4 else 576
-            stripe = trow[slot, :, 1152 * m : 1152 * m + width].astype(F32)
-            return stripe[:, V * q : V * q + V]
-
-        return load
-
     load_w.wait()
 
     def mixed(slot):
-        load = bf16_piece(slot)
         for m in range(5):
-            split_cols(load, planes, m)
+            split_cols(lambda lo, hi: trow[slot, :, lo:hi].astype(F32), planes, m)
         for h in range(2):
             parts = []
             for j in range(8):
                 parts += take_j(planes, 8 * h + j, 0, 4 * AB)
             tm[:, 1152 * h : 1152 * h + 1152] = jnp.concatenate(parts, axis=1).astype(BF16)
         at = pl.multiple_of(slot * V, 8)
-        r3[pl.ds(at, V), :] = jnp.dot(tm[...], wv[...], preferred_element_type=F32)
+        r3[pl.ds(at, V), :] = lax.dot_general(
+            tm[...], wv[...], (((1,), (1,)), ((), ())), preferred_element_type=F32
+        )
 
     mixed(c)
 
     load_d.wait()
     for m in range(5):
-        split_cols(lambda m, q: d32[:, 1152 * m + V * q : 1152 * m + V * q + V], planes, m)
+        split_cols(lambda lo, hi: d32[:, lo:hi], planes, m)
     for cc in range(4):
         parts = []
         for j in range(4):
@@ -175,8 +181,10 @@
     mixed(c_z)
     mixed(c_y)
 
-    col_land[0].wait_recv()
-    col_copy[2].start()
+    @pl.when(x != z)
+    def _():
+        col_land[0].wait_recv()
+        col_copy[2].start()
 
     row_land[2].wait_recv()
     row_land[3].wait_recv()
@@ -195,38 +203,71 @@
             pp[V * i : V * i + V, 128 * b : 128 * b + n] = planes2[b, pl.ds(i, V, stride=4), :][:, 0:n]
     pt[...] = pp[...].T
 
-    load_vo.wait()
-    col_land[1].wait_recv()
-    col_land[2].wait_recv()
-    xq[...] = lax.dot_general(
-        vo[...], tcol[...].reshape(4 * RB, CB), (((1,), (1,)), ((), ())), preferred_element_type=F32
-    )
-    xqr[c] = xq[...]
+    p_copy = send(pt, pr, p_s.at[0], p_r.at[0], c, r)
+
+    @pl.when(r != c)
+    def _():
+        p_copy.start()
+
+    @pl.when(r == c)
+    def _():
+        pr[...] = pt[...]
+
+    for rr in range(4):
+
+        @pl.when(r != rr)
+        def _():
+            send(trow.at[0], tlad.at[rr], lad_s.at[rr], lad_r.at[rr], rr, c).wait_recv()
+
+    fwd = (
+        send(tlad.at[r_d], tcol.at[r_d], f_s.at[0], col_r.at[0], r_k, c),
+        send(tlad.at[r_x], tcol.at[r_x], f_s.at[1], col_r.at[2], r_k, c),
+    )
+
+    @pl.when(r == c)
+    def _():
+        for copy in fwd:
+            copy.start()
+        tcol[r_d] = tlad[r_d]
+        tcol[r_x] = tlad[r_x]
+
     q_copy = [send(xq, xqr.at[c], q_s.at[q], q_r.at[q], r, peer) for q, peer in enumerate(col_peers)]
-    for copy in q_copy:
-        copy.start()
-
-    p_copy = send(pt, pr, p_s.at[0], p_r.at[0], c, r)
-
-    @pl.when(r != c)
-    def _():
-        p_copy.start()
-
-    @pl.when(r == c)
-    def _():
-        pr[...] = pt[...]
-
-    for q, peer in enumerate(col_peers):
-        send(xq, xqr.at[peer], q_s.at[q], q_r.at[q], r, peer).wait_recv()
-    x_sum = (xqr[0] + xqr[1]) + (xqr[2] + xqr[3])
-    w_hole = oo_ref[...].astype(F32) + 0.5 * x_sum
-    wt[...] = w_hole.T.astype(BF16)
-
-    for rr in range(4):
-
-        @pl.when(r != rr)
-        def _():
-            send(trow.at[0], tlad.at[rr], lad_s.at[rr], lad_r.at[rr], rr, c).wait_recv()
+
+    def hole_x():
+        load_vo.wait()
+        col_land[1].wait_recv()
+
+        @pl.when(jnp.logical_and(x == z, r != c))
+        def _():
+            col_land[0].wait_recv()
+
+        @pl.when(r != c)
+        def _():
+            col_land[2].wait_recv()
+
+        xq[...] = lax.dot_general(
+            vo[...], tcol[...].reshape(4 * RB, CB), (((1,), (1,)), ((), ())), preferred_element_type=F32
+        )
+        xqr[c] = xq[...]
+        for copy in q_copy:
+            copy.start()
+
+    def w_copy(rr):
+        return send(wt.at[RB * rr : RB * rr + RB], wblk.at[r], w_s.at[rr], w_r.at[r], rr, c)
+
+    def hole_w():
+        load_oo.wait()
+        for q, peer in enumerate(col_peers):
+            send(xq, xqr.at[peer], q_s.at[q], q_r.at[q], r, peer).wait_recv()
+        x_sum = (xqr[0] + xqr[1]) + (xqr[2] + xqr[3])
+        w_hole = oo[...].astype(F32) + 0.5 * x_sum
+        wt[...] = w_hole.T.astype(BF16)
+        wblk[r] = wt[pl.ds(pl.multiple_of(r * RB, RB), RB), :]
+        for rr in range(4):
+
+            @pl.when(r != rr)
+            def _():
+                w_copy(rr).start()
 
     def d2_copy(n):
         return send(acc.at[n, 1 - k], d2r.at[n], dd_s.at[n], dd_r.at[n], r_k, c)
@@ -239,7 +280,6 @@
 
     load_tail.wait()
     part = jnp.dot(tlad[...].reshape(4 * RB, CB), vtail[...], preferred_element_type=F32)
-    part = part + jnp.dot(wt[...], trow[c, :, NCH * CW : CB], preferred_element_type=F32)
     for rr in range(4):
         acct[rr % 2, rr // 2] = part[RB * rr : RB * rr + RB]
     d2_tail.start()
@@ -254,14 +294,10 @@
     def ladder_step(n, carry):
         slot = n % 2
         load_v(n, slot).wait()
-        at = pl.multiple_of(n * CW, CW)
         for h in range(2):
             part = jnp.dot(
                 tlad[...].reshape(4 * RB, CB), vbuf[slot, :, 256 * h : 256 * h + 256], preferred_element_type=F32
             )
-            part = part + jnp.dot(
-                wt[...], trow[c, :, pl.ds(pl.multiple_of(at + 256 * h, 256), 256)], preferred_element_type=F32
-            )
             for rr in range(4):
                 acc[n, rr % 2, rr // 2, :, 256 * h : 256 * h + 256] = part[RB * rr : RB * rr + RB]
         d2_copy(n).start()
@@ -281,23 +317,42 @@
         def _():
             second(n - 1)
 
+        @pl.when(n == 2)
+        def _():
+            hole_x()
+
+        @pl.when(n == 5)
+        def _():
+            hole_w()
+
         return carry
 
     lax.fori_loop(0, NCH, ladder_step, 0)
     second(NCH - 1)
 
     l_copy = []
+    for rr in range(4):
+
+        @pl.when(r != rr)
+        def _():
+            send(wt.at[0:RB], wblk.at[rr], w_s.at[rr], w_r.at[rr], rr, c).wait_recv()
+
+    wf[...] = jnp.concatenate([wblk[rr].astype(F32) for rr in range(4)], axis=1).astype(BF16)
+
+    def close(lo, hi, landed):
+        hole = jnp.dot(wf[...], tcol[:, :, lo:hi].reshape(4 * RB, hi - lo), preferred_element_type=F32)
+        r1[:, lo:hi] = r1[:, lo:hi] + landed + hole + vo[:, lo:hi].astype(F32)
+
     xx_tail.wait_recv()
-    r1[:, NCH * CW : CB] += xrt[...] + vo[:, NCH * CW : CB].astype(F32)
+    close(NCH * CW, CB, xrt[...])
     done = 0
     for m in range(5):
         width = 1152 if m < 4 else 576
         while done < NCH and CW * done < 1152 * m + width:
             xx_copy(done).wait_recv()
-            at = CW * done
-            r1[:, at : at + CW] += xrb[done] + vo[:, at : at + CW].astype(F32)
+            close(CW * done, CW * done + CW, xrb[done])
             done += 1
-        split_cols(lambda m, q: r1[:, 1152 * m + V * q : 1152 * m + V * q + V], planes, m)
+        split_cols(lambda lo, hi: r1[:, lo:hi], planes, m)
         rows = width // V * 4
         first = 32 * m
         for cc in range(4):
@@ -339,13 +394,28 @@
             top = planes[0, pl.ds(i, V, stride=4), :][:, 0:n] + pp[rows, cols]
             out_ref[rows, cols] = top / planes2[b, pl.ds(i, V, stride=4), :][:, 0:n]
 
-    for copy in (*row_copy, *col_copy, *q_copy, *d_copy, *l_copy, d2_tail, xx_tail):
+    for copy in (*row_copy, col_copy[1], *q_copy, *d_copy, *l_copy, d2_tail, xx_tail):
         copy.wait_send()
+
+    @pl.when(x == z)
+    def _():
+        col_copy[0].wait_send()
+
+    @pl.when(x != z)
+    def _():
+        col_copy[2].wait_send()
+
+    @pl.when(r == c)
+    def _():
+        for copy in fwd:
+            copy.wait_send()
+
     for slot in range(4):
 
         @pl.when(slot != r)
         def _():
             lad_copy(slot).wait_send()
+            w_copy(slot).wait_send()
 
     @pl.when(r != c)
     def _():
@@ -363,27 +433,27 @@
     vm = pltpu.VMEM
     dma = pltpu.SemaphoreType.DMA
     scratch = [
-        vm((RB, CB), F32), vm((RB, CB), F32), vm((RB, CB), BF16), vm((O * V, PB), BF16),
+        vm((RB, CB), F32), vm((RB, CB), F32), vm((RB, CB), BF16), vm((PB, O * V), BF16),
         vm((4, RB, CB), BF16), vm((4, RB, CB), BF16), vm((4, RB, CB), BF16),
         vm((2, AB * RB, 128), F32), vm((V, O * V), BF16),
         vm((PB, PB), F32), vm((PB, PB), F32), vm((PB, PB), F32), vm((PB, PB), F32),
         vm((4, V, PB), F32), vm((PB, PB), F32), vm((4, V, PB), F32), vm((PB, PB), F32),
         vm((5, PB, 128), F32),
-        vm((RB, O * O), F32), vm((4, RB, O * O), F32), vm((O * O, RB), BF16),
+        vm((RB, O * O), F32), vm((4, RB, O * O), F32), vm((O * O, RB), BF16), vm((RB, O * O), BF16), vm((4, RB, RB), BF16), vm((RB, O * O), BF16),
         vm((2, CB, CW), BF16), vm((CB, TW), BF16),
         vm((NCH, 2, 2, RB, CW), F32), vm((NCH, 2, RB, CW), F32), vm((NCH, RB, CW), F32), vm((NCH, RB, CW), F32),
         vm((2, 2, RB, TW), F32), vm((2, RB, TW), F32), vm((RB, TW), F32), vm((RB, TW), F32),
         vm((RB, CB), F32),
-        dma((5,)), dma((2,)), dma((4,)), dma((4,)), dma((3,)), dma((3,)), dma((4,)), dma((4,)), dma((3,)), dma((3,)),
+        dma((6,)), dma((2,)), dma((4,)), dma((4,)), dma((3,)), dma((3,)), dma((4,)), dma((4,)), dma((3,)), dma((3,)),
         dma((3,)), dma((3,)), dma((5, 3)), dma((5, 3)), dma((1,)), dma((1,)),
-        dma((NCH + 1,)), dma((NCH + 1,)), dma((NCH + 1,)), dma((NCH + 1,)),
+        dma((NCH + 1,)), dma((NCH + 1,)), dma((NCH + 1,)), dma((NCH + 1,)), dma((4,)), dma((4,)), dma((2,)),
     ]
     hbm = pl.BlockSpec(memory_space=pl.ANY)
     vmem = pl.BlockSpec(memory_space=pltpu.VMEM)
     call = pl.pallas_call(
         kernel,
         out_shape=jax.ShapeDtypeStruct((PB, PB), F32),
-        in_specs=[hbm, hbm, hbm, hbm, vmem, hbm],
+        in_specs=[hbm] * 6,
         out_specs=vmem,
         scratch_shapes=scratch,
         compiler_params=pltpu.CompilerParams(
@@ -391,10 +461,13 @@
         ),
         name="sweep",
     )
+    def local_sweep(t_blk, d_blk, voovv_blk, vvvvv_blk, oooo, w_blk):
+        return call(t_blk, d_blk, voovv_blk, vvvvv_blk, oooo, w_blk.T)
+
     return jax.shard_map(
-        call,
+        local_sweep,
         mesh=mesh,
-        in_specs=(P("row", "col"), P("row", "col"), P("row", "col"), P("row", "col"), P("row", None), P(None, "col")),
+        in_specs=(P("row", "col"), P("row", "col"), P("row", "col"), P("row", "col"), P(None, None), P(None, "col")),
         out_specs=P("row", "col"),
         check_vma=False,
     )

time: 129 us -> 117 us (0.907)
  local copies, waits for them, and re-layouts: 9.7 us -> 2.58 us
  Pallas kernels: 118 us -> 114 us
    unnamed x2 -> x1, local copies, waits for them, and re-layouts: 7.08 us -> 2.58 us
    pallas_call x1, Pallas kernels: 118 us -> 114 us  [local_sweep(): return call(t_blk, d_blk, voovv_blk, vvvvv_blk, oooo, w_blk.T)]
    another operation x2 -> x0, local copies, waits for them, and re-layouts: 2.62 us -> none
where the time goes in v2:
time: 117 us
  Pallas kernels  114 us (97%)
  local copies, waits for them, and re-layouts  2.58 us (2%)
    pallas_call x1, Pallas kernels, local_sweep(): return call(t_blk, d_blk, voovv_blk, vvvvv_blk, oooo, w_blk.T)  114 us
    unnamed x1, local copies, waits for them, and re-layouts  2.58 us

profile of v2, /device:TPU:0, one launch (start us, length us, event | category | flops | bytes accessed | tf_op | source)
XLA Modules:
  0.0 116.6 jit_solution(7661735917271060067)
XLA Ops:
  0.0 114.0 %sweep.1 = f32[576,576]{1,0:T(8,128)} custom-call(f32[64,5184]{1,0:T(8,128)} %t_hbm.1, f32[64,5184]{1,0:T(8,128)} %d_hbm.1, bf16[64,5184]{1,0:T(8,128)(2,1)} %vo_hbm.1, bf16[5184,5184]{1,0:T(8,128)(2,1)} %vv_hbm.1, bf16[256,256]{1,0:T(8,128)(2,1)} %oo_hbm.1, bf16[576,2304]{1,0:T(8,128)(2,1)} %bitcast.1), custom_call_target="tpu_custom_call" | custom-call | tf_op jit(solution)/shard_map/sweep/pallas_call | solution.py:465
  114.0 2.6 %copy.8 = f32[576,576]{1,0:T(8,128)} copy(f32[576,576]{1,0:T(8,128)} %sweep.1) | data formatting | bytes 2654208

commit v3 on v2

--- a/solution.py
+++ b/solution.py
@@ -46,10 +46,10 @@
 def kernel(
     t_hbm, d_hbm, vo_hbm, vv_hbm, oo_hbm, w_hbm, out_ref,
     t32, d32, vo, wv, trow, tcol, tlad, planes, tm, r3, pp, pt, pr,
-    dsnd, drcv, lsnd, lrcv, planes2, xq, xqr, wt, oo, wblk, wf, vbuf, vtail,
+    dsnd, drcv, lsnd, lrcv, planes2, prel, xq, xqr, wt, oo, wblk, wf, vbuf, vtail,
     acc, d2r, xsb, xrb, acct, d2t, xst, xrt, r1,
     in_sem, v_sem, row_s, row_r, col_s, col_r, lad_s, lad_r, q_s, q_r,
-    d_s, d_r, l_s, l_r, p_s, p_r, dd_s, dd_r, xx_s, xx_r, w_s, w_r, f_s,
+    d_s, d_r, l_s, l_r, p_s, p_r, fw_s, dd_s, dd_r, xx_s, xx_r, w_s, w_r, f_s,
 ):
     r = lax.axis_index("row")
     c = lax.axis_index("col")
@@ -99,50 +99,45 @@
     pl.semaphore_wait(barrier, 16)
 
     half = RB // 2
-    row_copy = (
-        send(trow.at[c], trow.at[c], row_s.at[0], row_r.at[0], r, c_y),
-        send(trow.at[c], trow.at[c], row_s.at[1], row_r.at[1], r, c_z),
-        send(trow.at[c_z, 0:half], trow.at[c_z, 0:half], row_s.at[2], row_r.at[2], r, c_y),
-        send(trow.at[c_y, half:RB], trow.at[c_y, half:RB], row_s.at[3], row_r.at[3], r, c_z),
-    )
-    row_land = (
-        send(trow.at[c_y], trow.at[c_y], row_s.at[0], row_r.at[0], r, c_y),
-        send(trow.at[c_z], trow.at[c_z], row_s.at[1], row_r.at[1], r, c_z),
-        send(trow.at[c_d, 0:half], trow.at[c_d, 0:half], row_s.at[2], row_r.at[2], r, c_y),
-        send(trow.at[c_d, half:RB], trow.at[c_d, half:RB], row_s.at[3], row_r.at[3], r, c_z),
-    )
-    col_copy = (
-        send(tcol.at[r], tcol.at[r], col_s.at[0], col_r.at[0], r_x, c),
-        send(tcol.at[r], tcol.at[r], col_s.at[1], col_r.at[1], r_k, c),
-        send(tcol.at[r_x], tcol.at[r_x], col_s.at[2], col_r.at[2], r_k, c),
-    )
-    col_land = (
-        send(tcol.at[r_x], tcol.at[r_x], col_s.at[0], col_r.at[0], r_x, c),
-        send(tcol.at[r_k], tcol.at[r_k], col_s.at[1], col_r.at[1], r_k, c),
-        send(tcol.at[r_d], tcol.at[r_d], col_s.at[2], col_r.at[2], r_k, c),
-    )
-    row_copy[0].start()
-    row_copy[1].start()
+    halves = (slice(0, half), slice(half, RB))
+
+    def row_copy(way, h):
+        block, peer = ((c, c_y), (c, c_z), ((c_z, c_y), (c_y, c_z))[h])[way]
+        piece = trow.at[block, halves[h]]
+        return send(piece, piece, row_s.at[way, h], row_r.at[way, h], r, peer)
+
+    def row_wait(way, h):
+        piece = trow.at[(c_y, c_z, c_d)[way], halves[h]]
+        send(piece, piece, row_s.at[way, h], row_r.at[way, h], r, c_y).wait_recv()
+
+    def col_piece(h):
+        piece = tcol.at[r, halves[h]]
+        return send(piece, piece, col_s.at[h], col_r.at[h], r_x, c)
+
+    col_pair = send(tcol.at[r], tcol.at[r], col_s.at[2], col_r.at[2], r_k, c)
+    col_relay = send(tcol.at[r_x], tcol.at[r_x], col_s.at[3], col_r.at[3], r_k, c)
+
+    def lad_copy(slot, h):
+        return send(trow.at[slot, halves[h]], tlad.at[r, halves[h]], lad_s.at[slot, h], lad_r.at[r, h], slot, c)
+
+    def dispatch(slot, h):
+        @pl.when(slot != r)
+        def _():
+            lad_copy(slot, h).start()
+
+        @pl.when(slot == r)
+        def _():
+            tlad[r, halves[h]] = trow[slot, halves[h]]
 
     @pl.when(x == z)
     def _():
-        col_copy[0].start()
-
-    col_copy[1].start()
-
-    def lad_copy(slot):
-        return send(trow.at[slot], tlad.at[r], lad_s.at[slot], lad_r.at[r], slot, c)
-
-    def dispatch(slot):
-        @pl.when(slot != r)
-        def _():
-            lad_copy(slot).start()
-
-        @pl.when(slot == r)
-        def _():
-            tlad[r] = trow[slot]
-
-    dispatch(c)
+        col_piece(0).start()
+
+    for h in range(2):
+        row_copy(0, h).start()
+        row_copy(1, h).start()
+        dispatch(c, h)
+    col_pair.start()
 
     load_w.wait()
 
@@ -161,6 +156,12 @@
 
     mixed(c)
 
+    row_wait(1, 0)
+    row_copy(2, 0).start()
+    dispatch(c_z, 0)
+    row_wait(0, 0)
+    dispatch(c_y, 0)
+
     load_d.wait()
     for m in range(5):
         split_cols(lambda lo, hi: d32[:, lo:hi], planes, m)
@@ -172,29 +173,29 @@
     own_rows = pl.ds(pl.multiple_of(c * V, 8), V)
     drcv[own_rows, :] = dsnd[c]
 
-    row_land[1].wait_recv()
-    row_copy[2].start()
-    dispatch(c_z)
-    row_land[0].wait_recv()
-    row_copy[3].start()
-    dispatch(c_y)
+    row_wait(1, 1)
+    dispatch(c_z, 1)
+    row_wait(0, 1)
+    row_copy(2, 1).start()
+    dispatch(c_y, 1)
     mixed(c_z)
+    row_wait(2, 0)
+    row_wait(2, 1)
+
+    @pl.when(x != z)
+    def _():
+        dispatch(c_d, 0)
+        dispatch(c_d, 1)
+
+    @pl.when(x == z)
+    def _():
+        col_piece(1).start()
+
     mixed(c_y)
-
-    @pl.when(x != z)
-    def _():
-        col_land[0].wait_recv()
-        col_copy[2].start()
-
-    row_land[2].wait_recv()
-    row_land[3].wait_recv()
-    dispatch(c_d)
+    mixed(c_d)
     d_copy = [
         send(dsnd.at[peer], drcv.at[own_rows], d_s.at[q], d_r.at[q], r, peer) for q, peer in enumerate(col_peers)
     ]
-    for copy in d_copy:
-        copy.start()
-    mixed(c_d)
 
     for b in range(5):
         n = 128 if b < 4 else 64
@@ -203,9 +204,18 @@
             pp[V * i : V * i + V, 128 * b : 128 * b + n] = planes2[b, pl.ds(i, V, stride=4), :][:, 0:n]
     pt[...] = pp[...].T
 
+    top, low = slice(0, PB // 2), slice(PB // 2, PB)
     p_copy = send(pt, pr, p_s.at[0], p_r.at[0], c, r)
-
-    @pl.when(r != c)
+    p_out = (
+        send(pt.at[top], prel.at[0], p_s.at[1], p_r.at[1], r_x, c),
+        send(pt.at[low], prel.at[1], p_s.at[2], p_r.at[2], r, c_z),
+    )
+    p_on = (
+        send(prel.at[0], pr.at[top], p_s.at[3], p_r.at[3], c, r_x),
+        send(prel.at[1], pr.at[low], p_s.at[4], p_r.at[4], c_z, r),
+    )
+
+    @pl.when(jnp.logical_and(x == z, r != c))
     def _():
         p_copy.start()
 
@@ -213,15 +223,32 @@
     def _():
         pr[...] = pt[...]
 
-    for rr in range(4):
-
-        @pl.when(r != rr)
-        def _():
-            send(trow.at[0], tlad.at[rr], lad_s.at[rr], lad_r.at[rr], rr, c).wait_recv()
+    @pl.when(x != z)
+    def _():
+        p_out[1].start()
+        p_out[0].start()
+
+    def lad_wait(slot, h):
+        send(trow.at[0, halves[h]], tlad.at[slot, halves[h]], lad_s.at[slot, h], lad_r.at[slot, h], r, c).wait_recv()
+
+    def lad_forward(slot, h):
+        piece = tlad.at[slot, halves[h]]
+        return send(piece, piece, fw_s.at[slot, h], lad_r.at[slot, h], r, c_y)
+
+    gives = jnp.logical_and(x != z, k == y)
+    for h in range(2):
+        lad_wait(r_k, h)
+    for h in range(2):
+        for slot in (r_x, r_d):
+            lad_wait(slot, h)
+
+            @pl.when(gives)
+            def _():
+                lad_forward(slot, h).start()
 
     fwd = (
-        send(tlad.at[r_d], tcol.at[r_d], f_s.at[0], col_r.at[0], r_k, c),
-        send(tlad.at[r_x], tcol.at[r_x], f_s.at[1], col_r.at[2], r_k, c),
+        send(tlad.at[r_d], tcol.at[r_d], f_s.at[0], col_r.at[4], r_k, c),
+        send(tlad.at[r_x], tcol.at[r_x], f_s.at[1], col_r.at[3], r_k, c),
     )
 
     @pl.when(r == c)
@@ -235,15 +262,15 @@
 
     def hole_x():
         load_vo.wait()
-        col_land[1].wait_recv()
+        send(tcol.at[r_k], tcol.at[r_k], col_s.at[2], col_r.at[2], r_k, c).wait_recv()
 
         @pl.when(jnp.logical_and(x == z, r != c))
         def _():
-            col_land[0].wait_recv()
+            send(tcol.at[r_x], tcol.at[r_x], f_s.at[0], col_r.at[4], r_k, c).wait_recv()
 
         @pl.when(r != c)
         def _():
-            col_land[2].wait_recv()
+            send(tcol.at[r_d], tcol.at[r_d], col_s.at[3], col_r.at[3], r_k, c).wait_recv()
 
         xq[...] = lax.dot_general(
             vo[...], tcol[...].reshape(4 * RB, CB), (((1,), (1,)), ((), ())), preferred_element_type=F32
@@ -317,11 +344,29 @@
         def _():
             second(n - 1)
 
-        @pl.when(n == 2)
+        @pl.when(n == 0)
+        def _():
+            for copy in d_copy:
+                copy.start()
+
+        @pl.when(jnp.logical_and(n == 2, x != z))
+        def _():
+            for h in range(2):
+                piece = tcol.at[r_x, halves[h]]
+                send(piece, piece, col_s.at[h], col_r.at[h], r_x, c).wait_recv()
+            col_relay.start()
+
+        @pl.when(n == 3)
         def _():
             hole_x()
 
-        @pl.when(n == 5)
+        @pl.when(jnp.logical_and(n == 4, x == z))
+        def _():
+            for copy, on in zip(p_out, p_on):
+                copy.wait_recv()
+                on.start()
+
+        @pl.when(n == 6)
         def _():
             hole_w()
 
@@ -369,9 +414,14 @@
             copy.start()
             l_copy.append(copy)
 
-    @pl.when(r != c)
+    @pl.when(jnp.logical_and(x == z, r != c))
     def _():
         p_copy.wait_recv()
+
+    @pl.when(x != z)
+    def _():
+        for copy in p_on:
+            copy.wait_recv()
 
     pp[...] = pp[...] + pr[...]
     for q, peer in enumerate(col_peers):
@@ -394,32 +444,50 @@
             top = planes[0, pl.ds(i, V, stride=4), :][:, 0:n] + pp[rows, cols]
             out_ref[rows, cols] = top / planes2[b, pl.ds(i, V, stride=4), :][:, 0:n]
 
-    for copy in (*row_copy, col_copy[1], *q_copy, *d_copy, *l_copy, d2_tail, xx_tail):
+    for copy in (col_pair, *q_copy, *d_copy, *l_copy, d2_tail, xx_tail):
         copy.wait_send()
+    for way in range(3):
+        for h in range(2):
+            row_copy(way, h).wait_send()
 
     @pl.when(x == z)
     def _():
-        col_copy[0].wait_send()
+        for h in range(2):
+            col_piece(h).wait_send()
+        for copy in p_on:
+            copy.wait_send()
+
+    @pl.when(jnp.logical_and(x == z, r != c))
+    def _():
+        p_copy.wait_send()
 
     @pl.when(x != z)
     def _():
-        col_copy[2].wait_send()
+        col_relay.wait_send()
+        for copy in p_out:
+            copy.wait_send()
 
     @pl.when(r == c)
     def _():
         for copy in fwd:
             copy.wait_send()
 
+    @pl.when(gives)
+    def _():
+        for h in range(2):
+            for slot in (r_x, r_d):
+                lad_forward(slot, h).wait_send()
+
     for slot in range(4):
 
         @pl.when(slot != r)
         def _():
-            lad_copy(slot).wait_send()
             w_copy(slot).wait_send()
 
-    @pl.when(r != c)
-    def _():
-        p_copy.wait_send()
+        @pl.when(jnp.logical_and(slot != r, jnp.logical_or(slot != c_d, x != z)))
+        def _():
+            for h in range(2):
+                lad_copy(slot, h).wait_send()
 
     def drain(n, carry):
         d2_copy(n).wait_send()
@@ -438,14 +506,14 @@
         vm((2, AB * RB, 128), F32), vm((V, O * V), BF16),
         vm((PB, PB), F32), vm((PB, PB), F32), vm((PB, PB), F32), vm((PB, PB), F32),
         vm((4, V, PB), F32), vm((PB, PB), F32), vm((4, V, PB), F32), vm((PB, PB), F32),
-        vm((5, PB, 128), F32),
+        vm((5, PB, 128), F32), vm((2, PB // 2, PB), F32),
         vm((RB, O * O), F32), vm((4, RB, O * O), F32), vm((O * O, RB), BF16), vm((RB, O * O), BF16), vm((4, RB, RB), BF16), vm((RB, O * O), BF16),
         vm((2, CB, CW), BF16), vm((CB, TW), BF16),
         vm((NCH, 2, 2, RB, CW), F32), vm((NCH, 2, RB, CW), F32), vm((NCH, RB, CW), F32), vm((NCH, RB, CW), F32),
         vm((2, 2, RB, TW), F32), vm((2, RB, TW), F32), vm((RB, TW), F32), vm((RB, TW), F32),
         vm((RB, CB), F32),
-        dma((6,)), dma((2,)), dma((4,)), dma((4,)), dma((3,)), dma((3,)), dma((4,)), dma((4,)), dma((3,)), dma((3,)),
-        dma((3,)), dma((3,)), dma((5, 3)), dma((5, 3)), dma((1,)), dma((1,)),
+        dma((6,)), dma((2,)), dma((3, 2)), dma((3, 2)), dma((5,)), dma((5,)), dma((4, 2)), dma((4, 2)),
+        dma((3,)), dma((3,)), dma((3,)), dma((3,)), dma((5, 3)), dma((5, 3)), dma((5,)), dma((5,)), dma((4, 2)),
         dma((NCH + 1,)), dma((NCH + 1,)), dma((NCH + 1,)), dma((NCH + 1,)), dma((4,)), dma((4,)), dma((2,)),
     ]
     hbm = pl.BlockSpec(memory_space=pl.ANY)

time: 117 us -> 111 us (0.949)
  Pallas kernels: 114 us -> 108 us
    pallas_call x1, Pallas kernels: 114 us -> 108 us  [local_sweep(): return call(t_blk, d_blk, voovv_blk, vvvvv_blk, oooo, w_blk.T)]
where the time goes in v3:
time: 111 us
  Pallas kernels  108 us (97%)
  local copies, waits for them, and re-layouts  2.58 us (2%)
    pallas_call x1, Pallas kernels, local_sweep(): return call(t_blk, d_blk, voovv_blk, vvvvv_blk, oooo, w_blk.T)  108 us
    unnamed x1, local copies, waits for them, and re-layouts  2.58 us

profile of v3, /device:TPU:0, one launch (start us, length us, event | category | flops | bytes accessed | tf_op | source)
XLA Modules:
  0.0 110.7 jit_solution(13069887391804193326)
XLA Ops:
  0.0 108.1 %sweep.1 = f32[576,576]{1,0:T(8,128)} custom-call(f32[64,5184]{1,0:T(8,128)} %t_hbm.1, f32[64,5184]{1,0:T(8,128)} %d_hbm.1, bf16[64,5184]{1,0:T(8,128)(2,1)} %vo_hbm.1, bf16[5184,5184]{1,0:T(8,128)(2,1)} %vv_hbm.1, bf16[256,256]{1,0:T(8,128)(2,1)} %oo_hbm.1, bf16[576,2304]{1,0:T(8,128)(2,1)} %bitcast.1), custom_call_target="tpu_custom_call" | custom-call | tf_op jit(solution)/shard_map/sweep/pallas_call | solution.py:533
  108.1 2.6 %copy.8 = f32[576,576]{1,0:T(8,128)} copy(f32[576,576]{1,0:T(8,128)} %sweep.1) | data formatting | bytes 2654208
